TPU v7x, 32 devices: a whole 2x2x4 slice. The times are simulated.
32 devices in a mesh: train: 2 (over y), tp: 8 (over z, x), dp: 2 (over core).
Axes of the slice: x: 2, y: 2, z: 4, core: 2. Of those that a mesh axis runs over, the one named last changes fastest.
Arguments:
- adapter_down_factor: bfloat16 [2, 2, 64, 8192], P(None, None, None, ('train', 'tp')), may hold values from -6 to 6
- adapter_up_factor: bfloat16 [2, 2, 1024, 64], P(None, None, ('train', 'tp')), may hold values from -0.75 to 0.75
- projection_weight: bfloat16 [2, 2, 1024, 8192], P(None, None, 'tp'), may hold values from -6 to 6
Outputs:
- merged: bfloat16 [2, 2, 1024, 8192], P(None, None, 'tp')
All inputs are finite; a program needn't handle non-finite values.
Results may differ from a plain program's by a relative error of at most 0.001.
Values may be sent and summed in bfloat16 or wider, within the bound.
A program may use at most 64 MiB of HBM per device.

v0:
```python
import jax
import jax.numpy as jnp
from jax import lax
from jax.sharding import PartitionSpec as P

adapter_scale = 2.0


def per_device(adapter_down_factor, adapter_up_factor, projection_weight):
    per_rows = projection_weight.shape[2]
    all_up_factors = lax.all_gather(adapter_up_factor, ("train", "tp"), axis=2, tiled=True)
    offset = lax.axis_index("tp") * per_rows
    b_rows = lax.dynamic_slice_in_dim(all_up_factors, offset, per_rows, 2)
    weight_block = projection_weight.astype(jnp.float32)
    weight_update = jnp.einsum(
        "eitd,eidh->eith",
        b_rows,
        lax.all_gather(adapter_down_factor, ("train", "tp"), axis=3, tiled=True),
        preferred_element_type=jnp.float32,
    )
    return (weight_block + adapter_scale * weight_update).astype(jnp.bfloat16)


def solution(mesh):
    in_specs = (
        P(None, None, None, ("train", "tp")),
        P(None, None, ("train", "tp"), None),
        P(None, None, "tp", None),
    )
    out_specs = P(None, None, "tp", None)
    return jax.shard_map(
        per_device, mesh=mesh, in_specs=in_specs, out_specs=out_specs, check_vma=False
    )
```

profile of v0, /device:TPU:0, one launch (start us, length us, event | category | flops | bytes accessed | tf_op | source)
XLA Modules:
  0.0 113.6 jit_solution(2396535174543031142)
XLA Ops:
  6.5 0.0 all-gather.2.cloned.1.call-start
  6.5 0.7 all-gather.2.cloned.1.call-update
  7.3 0.9 copy.5
  8.2 51.4 %all_gather.6 = bf16[2,2,1024,64]{3,1,0,2:T(2,128)(2,1)S(1)} all-gather(bf16[2,2,64,64]{3,1,0,2:T(2,128)(2,1)S(1)} %copy.5), channel_id=1, replica_groups=mesh['train'=2,'tp'=8,'dp'=2] {'train','tp'}, dimensions={2}, use_global_device_ids=true | all-gather | bytes 557056 | tf_op jit(solution)/shard_map/all_gather | solution.py:11
  59.5 0.1 constant_dynamic-slice_fusion
  59.6 39.0 %all-gather.2.cloned.1.call-done = bf16[2,2,64,8192]{3,2,1,0:T(8,128)(2,1)} async-done(((bf16[2,2,64,512]{3,2,1,0:T(8,128)(2,1)}), bf16[2,2,64,8192]{3,2,1,0:T(8,128)(2,1)}) %all-gather.2.cloned.1.call-update) | async-done | bytes 4194320 | tf_op jit(solution)/shard_map/all_gather | solution.py:18
  98.6 8.2 %add_convert_fusion = bf16[2,2,128,8192]{3,2,1,0:T(8,128)(2,1)} fusion(bf16[2,2,128,8192]{3,2,1,0:T(8,128)(2,1)} %param.5, bf16[2,2,64,8192]{3,2,1,0:T(8,128)(2,1)} %all-gather.2.cloned.1.call-done, bf16[2,2,128,64]{3,1,0,2:T(2,128)(2,1)S(1)} %constant_dynamic-slice_fusion), kind=kOutput, calls=%fused_computation | convolution fusion | flops 553648128 | bytes 21037056 | tf_op jit(solution)/shard_map/eitd,eidh->eith/dot_general | solution.py:15
Async XLA Ops:
  6.5 92.0 %all-gather.2.cloned.1.call-start = ((), (), s32[]{:S(2)}) async-start(), calls=%async_computation | async-start | bytes 4456448 | tf_op jit(solution)/shard_map/all_gather | solution.py:18
Sparse Core Ops, SparseCore 0:
  10.1 88.4 all-gather.1
where the time goes:
time: 114 us
  blocking collectives  51.4 us (45%)
  waiting for transfers between devices  39.7 us (35%)
  between operations  13.4 us (12%)
  matrix products  8.17 us (7%)
    all_gather x1, blocking collectives, per_device(): lax.all_gather(adapter_up_factor, ('train', 'tp'), axis=2, tiled=True)  51.4 us
    all_gather x1, waiting for transfers between devices, per_device(): lax.all_gather(adapter_down_factor, ('train', 'tp'), axis=3, tiled=True)  39 us
    dot_general x1, matrix products, per_device(): jnp.einsum('eitd,eidh->eith', b_rows, lax.all_gather(adapter_down_factor,...  8.17 us
  transfers between devices with their start and end apart: 1, of which 1 were waited for; matrix products, arithmetic and copies ran while one was open for 1% of the time, Pallas kernels for 0%

commit v1 on v0

v1 whole, which is shorter than its diff:
```python
import functools

import jax
import jax.numpy as jnp
from jax import lax
from jax.experimental import pallas as pl
from jax.experimental.pallas import tpu as pltpu
from jax.sharding import PartitionSpec as P

adapter_scale = 2.0
MESH = pl.DeviceIdType.MESH


def place(train, tp, dp):
    return {"train": train, "tp": tp, "dp": dp}


def nearest(z, depth, j):
    if j == 0:
        return z
    low = jnp.minimum(z, depth - 1 - z)
    side = jnp.where(2 * z < depth - 1, 1, -1)
    near = z + side * ((j + 1) // 2) * (1 if j % 2 else -1)
    far = z + side * (j - low)
    return jnp.where(j <= 2 * low, near, far)


def gather_merge(
    tp, train, layers, kinds,
    down_ref, up_ref, weight_ref, out_ref,
    downs, ups, recv_sem, pass_recv, link_sem, line_sem, pass_sem, up_send, up_recv, weight_sem,
):
    y = lax.axis_index("train")
    t = lax.axis_index("tp")
    core = lax.axis_index("dp")
    depth = tp // 2
    z, x = t // 2, t % 2
    columns = down_ref.shape[-1]
    up_rows = up_ref.shape[2]
    other = 1 - core

    weight_copy = pltpu.make_async_copy(weight_ref, out_ref, weight_sem)
    weight_copy.start()

    def device(yy, zz, xx):
        return place(yy, zz * 2 + xx, core)

    to_x = device(y, z, 1 - x)
    to_y = device(1 - y, z, x)
    partner = place(y, t, other)

    group = y * tp + t
    up_target = group // train
    up_slot = group % train

    barrier = pltpu.get_barrier_semaphore()

    def greet(where):
        pl.semaphore_signal(barrier, inc=1, device_id=where, device_id_type=MESH)

    greet(to_x)
    greet(to_y)
    greet(partner)

    @pl.when(z > 0)
    def _():
        greet(device(y, z - 1, x))

    @pl.when(z < depth - 1)
    def _():
        greet(device(y, z + 1, x))

    for j in range(train):
        source = t * train + j

        @pl.when(source != group)
        def _():
            greet(place(source // tp, source % tp, core))

    peers = 3 + jnp.where(z > 0, 1, 0) + jnp.where(z < depth - 1, 1, 0)
    for yy in range(train):
        peers += jnp.where(yy * tp + up_target != group, 1, 0)
    pl.semaphore_wait(barrier, peers)

    def up_copy(yy):
        return pltpu.make_async_remote_copy(
            src_ref=up_ref, dst_ref=ups.at[up_slot],
            send_sem=up_send.at[yy], recv_sem=up_recv.at[up_slot],
            device_id=place(yy, up_target, core), device_id_type=MESH,
        )

    def index(yy, zz, xx, e, kind):
        return ((yy * tp + zz * 2 + xx) * layers + e) * kinds + kind

    def send(src, piece, where, sem):
        pltpu.make_async_remote_copy(
            src_ref=src, dst_ref=downs.at[piece], send_sem=sem,
            recv_sem=recv_sem.at[piece // (layers * kinds) * kinds + piece % kinds],
            device_id=where, device_id_type=MESH,
        ).start()

    def hand_over(piece):
        pltpu.make_async_remote_copy(
            src_ref=downs.at[piece], dst_ref=downs.at[piece], send_sem=pass_sem,
            recv_sem=pass_recv.at[piece // (layers * kinds) * kinds + piece % kinds],
            device_id=partner, device_id_type=MESH,
        ).start()

    def arrive(piece):
        sem = recv_sem.at[piece // (layers * kinds) * kinds + piece % kinds]
        pltpu.make_async_copy(downs.at[piece], downs.at[piece], sem).wait()

    x_sem, y_sem = link_sem.at[0], link_sem.at[1]

    for kind in range(kinds):
        piece = index(y, z, x, core, kind)
        mine = down_ref.at[core, kind]

        @pl.when(z > 0)
        def _():
            send(mine, piece, device(y, z - 1, x), line_sem.at[kind, z])

        @pl.when(z < depth - 1)
        def _():
            send(mine, piece, device(y, z + 1, x), line_sem.at[kind, depth])

        send(mine, piece, to_x, x_sem)
        send(mine, piece, to_y, y_sem)

    for yy in range(train):
        @pl.when(yy * tp + up_target != group)
        def _():
            up_copy(yy).start()

    for e in range(layers):
        for kind in range(kinds):
            downs[index(y, z, x, e, kind)] = down_ref[e, kind]

    def combine(yy, zz, xx, e, kind):
        block = downs[index(yy, zz, xx, e, kind)]
        at = pl.ds(pl.multiple_of((yy * tp + zz * 2 + xx) * columns, columns), columns)
        for j in range(train):
            rows = pl.ds(j * up_rows, up_rows)
            update = jnp.dot(
                ups[j, e, kind] * adapter_scale, block, preferred_element_type=jnp.float32
            )
            old = out_ref[e, kind, rows, at].astype(jnp.float32)
            out_ref[e, kind, rows, at] = (old + update).astype(out_ref.dtype)

    def merge(level):
        zz = nearest(z, depth, level)
        for yy in (y, 1 - y):
            for xx in (x, 1 - x):
                if level == 0 and yy is y and xx is x:
                    continue
                for kind in range(kinds):
                    piece = index(yy, zz, xx, other, kind)
                    sem = pass_recv.at[piece // (layers * kinds) * kinds + piece % kinds]
                    pltpu.make_async_copy(downs.at[piece], downs.at[piece], sem).wait()

        def step(i, carry):
            kind = i % kinds
            e = i // kinds % layers
            corner = i // (kinds * layers)
            combine(corner // 2, zz, corner % 2, e, kind)
            return carry

        lax.fori_loop(0, 4 * layers * kinds, step, 0)

    for step in range(depth + 3):
        for kind in range(kinds):
            first, second = (to_x, to_y) if kind == 0 else (to_y, to_x)
            first_sem, second_sem = (x_sem, y_sem) if kind == 0 else (y_sem, x_sem)
            flip_x = (1 - x, x) if kind == 0 else (x, 1 - x)
            flip_y = (y, 1 - y) if kind == 0 else (1 - y, y)
            if 1 <= step < depth:
                zz = nearest(z, depth, step)
                piece = index(y, zz, x, core, kind)
                arrive(piece)
                onward = jnp.where(zz > z, z - 1, z + 1)

                @pl.when(jnp.logical_and(onward >= 0, onward < depth))
                def _():
                    send(downs.at[piece], piece, device(y, onward, x), line_sem.at[kind, zz])

                send(downs.at[piece], piece, first, first_sem)
                send(downs.at[piece], piece, second, second_sem)
                hand_over(piece)
            if 1 <= step <= depth:
                zz = nearest(z, depth, step - 1)
                piece = index(flip_y[0], zz, flip_x[0], core, kind)
                arrive(piece)
                send(downs.at[piece], piece, second, second_sem)
                hand_over(piece)
        for kind in range(kinds):
            flip_x = (1 - x, x) if kind == 0 else (x, 1 - x)
            flip_y = (y, 1 - y) if kind == 0 else (1 - y, y)
            if 1 <= step <= depth:
                zz = nearest(z, depth, step - 1)
                piece = index(flip_y[1], zz, flip_x[1], core, kind)
                arrive(piece)
                hand_over(piece)
            if 2 <= step <= depth + 1:
                zz = nearest(z, depth, step - 2)
                piece = index(1 - y, zz, 1 - x, core, kind)
                arrive(piece)
                hand_over(piece)
        if step == 2:
            weight_copy.wait()
            for j in range(train):
                @pl.when(t * train + j != group)
                def _():
                    pltpu.make_async_copy(ups.at[j], ups.at[j], up_recv.at[j]).wait()

                @pl.when(t * train + j == group)
                def _():
                    ups[j] = up_ref[...]
        if step >= 3:
            merge(step - 3)

    for kind in range(kinds):
        for zz in range(depth):
            onward = jnp.where(zz > z, z - 1, z + 1)

            @pl.when(jnp.logical_and(zz != z, jnp.logical_and(onward >= 0, onward < depth)))
            def _():
                pltpu.make_async_copy(downs.at[0], downs.at[0], line_sem.at[kind, zz]).wait()

        @pl.when(z > 0)
        def _():
            pltpu.make_async_copy(downs.at[0], downs.at[0], line_sem.at[kind, z]).wait()

        @pl.when(z < depth - 1)
        def _():
            pltpu.make_async_copy(downs.at[0], downs.at[0], line_sem.at[kind, depth]).wait()

    over_link = downs.at[pl.ds(0, 3 * depth)]
    pltpu.make_async_copy(over_link, over_link, x_sem).wait()
    pltpu.make_async_copy(over_link, over_link, y_sem).wait()
    handed = downs.at[pl.ds(0, kinds * (4 * depth - 1))]
    pltpu.make_async_copy(handed, handed, pass_sem).wait()
    for yy in range(train):
        @pl.when(yy * tp + up_target != group)
        def _():
            up_copy(yy).wait_send()


def relayed(tp, train, down, up, weight):
    layers, kinds, rank, columns = down.shape
    holders = tp * train
    kernel = functools.partial(gather_merge, tp, train, layers, kinds)
    vmem = pl.BlockSpec(memory_space=pltpu.VMEM)
    return pl.pallas_call(
        kernel,
        out_shape=pltpu.VMEM(weight.shape, weight.dtype),
        in_specs=[vmem, vmem, pl.BlockSpec(memory_space=pl.ANY)],
        out_specs=vmem,
        scratch_shapes=[
            pltpu.VMEM((holders * layers * kinds, rank, columns), down.dtype),
            pltpu.VMEM((train,) + up.shape, up.dtype),
            pltpu.SemaphoreType.DMA((holders * kinds,)),
            pltpu.SemaphoreType.DMA((holders * kinds,)),
            pltpu.SemaphoreType.DMA((2,)),
            pltpu.SemaphoreType.DMA((kinds, tp // 2 + 1)),
            pltpu.SemaphoreType.DMA,
            pltpu.SemaphoreType.DMA((train,)),
            pltpu.SemaphoreType.DMA((train,)),
            pltpu.SemaphoreType.DMA,
        ],
        compiler_params=pltpu.CompilerParams(
            collective_id=0, has_side_effects=True, vmem_limit_bytes=40 * 1024 * 1024
        ),
        name="gather_merge",
    )(down, up, weight)


def gathered(down, up, weight):
    per_rows = weight.shape[2]
    all_up = lax.all_gather(up, ("train", "tp"), axis=2, tiled=True)
    rows = lax.dynamic_slice_in_dim(all_up, lax.axis_index("tp") * per_rows, per_rows, 2)
    update = jnp.einsum(
        "eitd,eidh->eith",
        rows,
        lax.all_gather(down, ("train", "tp"), axis=3, tiled=True),
        preferred_element_type=jnp.float32,
    )
    return (weight.astype(jnp.float32) + adapter_scale * update).astype(jnp.bfloat16)


def per_device(tp, train, dp, down, up, weight):
    layers, kinds = down.shape[:2]
    if train == 2 and tp % 2 == 0 and tp >= 4 and layers == dp == 2 and kinds == 2:
        return relayed(tp, train, down, up, weight)
    return gathered(down, up, weight)


def solution(mesh):
    in_specs = (
        P(None, None, None, ("train", "tp")),
        P(None, None, ("train", "tp"), None),
        P(None, None, "tp", None),
    )
    out_specs = P(None, None, "tp", None)
    sizes = [mesh.shape[axis] for axis in ("tp", "train", "dp")]
    return jax.shard_map(
        functools.partial(per_device, *sizes),
        mesh=mesh, in_specs=in_specs, out_specs=out_specs, check_vma=False,
    )
```

time: 114 us -> 41.3 us (0.36)
  blocking collectives: 51.4 us -> 0 us
  waiting for transfers between devices: 39.7 us -> 0 us
  Pallas kernels: 0 us -> 35.9 us
  between operations: 13.4 us -> 0.01 us
  matrix products: 8.17 us -> 0 us
  local copies, waits for them, and re-layouts: 1 us -> 5.19 us
    all_gather x1 -> x0, blocking collectives: 51.4 us -> none  [per_device(): lax.all_gather(adapter_up_factor, ('train', 'tp'), axis=2, tiled=True)]
    all_gather x1 -> x0, waiting for transfers between devices: 39 us -> none  [per_device(): lax.all_gather(adapter_down_factor, ('train', 'tp'), axis=3, tiled=True)]
    pallas_call x0 -> x1, Pallas kernels: none -> 35.9 us  [relayed(): pl.pallas_call(kernel, out_shape=pltpu.VMEM(weight.shape, weight.dtype),...]
    dot_general x1 -> x0, matrix products: 8.17 us -> none  [per_device(): jnp.einsum('eitd,eidh->eith', b_rows, lax.all_gather(adapter_down_factor,...]
    unnamed x1 -> x5, local copies, waits for them, and re-layouts: 0.91 us -> 5.19 us
  transfers between devices with their start and end apart: 1 -> 0, of which waited for: 1 -> 0; matrix products, arithmetic and copies ran while one was open for 1% -> 0% of each run, Pallas kernels for 0% -> 0%
where the time goes in v1:
time: 41.3 us; the launch traced here: 41.1 us
  Pallas kernels  35.9 us (87%)
  local copies, waits for them, and re-layouts  5.19 us (13%)
    pallas_call x1, Pallas kernels, relayed(): pl.pallas_call(kernel, out_shape=pltpu.VMEM(weight.shape, weight.dtype),...  35.9 us
    unnamed x5, local copies, waits for them, and re-layouts  5.19 us

profile of v1, /device:TPU:0, one launch (start us, length us, event | category | flops | bytes accessed | tf_op | source)
XLA Modules:
  0.0 41.1 jit_solution(16511020115423376804)
XLA Ops:
  0.0 0.0 copy-start
  0.0 0.9 %copy-done = bf16[2,2,64,512]{3,2,1,0:T(8,128)(2,1)S(1)} copy-done((bf16[2,2,64,512]{3,2,1,0:T(8,128)(2,1)S(1)}, bf16[2,2,64,512]{3,2,1,0:T(8,128)(2,1)}, u32[]{:S(2)}) %copy-start) | copy-done | bytes 262168
  1.0 0.0 copy-start.1
  1.0 0.8 %copy-done.1 = bf16[2,2,64,64]{3,2,1,0:T(8,128)(2,1)S(1)} copy-done((bf16[2,2,64,64]{3,2,1,0:T(8,128)(2,1)S(1)}, bf16[2,2,64,64]{3,2,1,0:T(8,128)(2,1)}, u32[]{:S(2)}) %copy-start.1) | copy-done | bytes 32792
  1.8 35.9 %gather_merge.1 = bf16[2,2,128,8192]{3,2,1,0:T(8,128)(2,1)S(1)} custom-call(bf16[2,2,64,512]{3,2,1,0:T(8,128)(2,1)S(1)} %copy-done, bf16[2,2,64,64]{3,2,1,0:T(8,128)(2,1)S(1)} %copy-done.1, bf16[2,2,128,8192]{3,2,1,0:T(8,128)(2,1)} %weight_ref.1), custom_call_target="tpu_custom_call" | custom-call | tf_op jit(solution)/shard_map/gather_merge/pallas_call | solution.py:253
  37.7 3.4 %copy.5 = bf16[2,2,128,8192]{3,2,1,0:T(8,128)(2,1)} copy(bf16[2,2,128,8192]{3,2,1,0:T(8,128)(2,1)S(1)} %gather_merge.1) | data formatting | bytes 16777216
Async XLA Ops:
  0.0 0.9 %copy-start = (bf16[2,2,64,512]{3,2,1,0:T(8,128)(2,1)S(1)}, bf16[2,2,64,512]{3,2,1,0:T(8,128)(2,1)}, u32[]{:S(2)}) copy-start(bf16[2,2,64,512]{3,2,1,0:T(8,128)(2,1)} %down_ref.1) | copy-start | bytes 786436
  1.0 0.8 %copy-start.1 = (bf16[2,2,64,64]{3,2,1,0:T(8,128)(2,1)S(1)}, bf16[2,2,64,64]{3,2,1,0:T(8,128)(2,1)}, u32[]{:S(2)}) copy-start(bf16[2,2,64,64]{3,2,1,0:T(8,128)(2,1)} %up_ref.1) | copy-start | bytes 98308

commit v2 on v1

--- a/solution.py
+++ b/solution.py
@@ -28,7 +28,7 @@
 def gather_merge(
     tp, train, layers, kinds,
     down_ref, up_ref, weight_ref, out_ref,
-    downs, ups, recv_sem, pass_recv, link_sem, line_sem, pass_sem, up_send, up_recv, weight_sem,
+    downs, ups, scaled, recv_sem, pass_recv, link_sem, line_sem, pass_sem, up_send, up_recv, weight_sem,
 ):
     y = lax.axis_index("train")
     t = lax.axis_index("tp")
@@ -139,13 +139,11 @@
     def combine(yy, zz, xx, e, kind):
         block = downs[index(yy, zz, xx, e, kind)]
         at = pl.ds(pl.multiple_of((yy * tp + zz * 2 + xx) * columns, columns), columns)
-        for j in range(train):
-            rows = pl.ds(j * up_rows, up_rows)
-            update = jnp.dot(
-                ups[j, e, kind] * adapter_scale, block, preferred_element_type=jnp.float32
-            )
-            old = out_ref[e, kind, rows, at].astype(jnp.float32)
-            out_ref[e, kind, rows, at] = (old + update).astype(out_ref.dtype)
+        update = jnp.dot(
+            scaled[e, kind], block, preferred_element_type=jnp.float32
+        )
+        old = out_ref[e, kind, :, at].astype(jnp.float32)
+        out_ref[e, kind, :, at] = (old + update).astype(out_ref.dtype)
 
     def merge(level):
         zz = nearest(z, depth, level)
@@ -165,7 +163,7 @@
             combine(corner // 2, zz, corner % 2, e, kind)
             return carry
 
-        lax.fori_loop(0, 4 * layers * kinds, step, 0)
+        lax.fori_loop(0, 4 * layers * kinds, step, 0, unroll=4)
 
     for step in range(depth + 3):
         for kind in range(kinds):
@@ -215,6 +213,8 @@
                 @pl.when(t * train + j == group)
                 def _():
                     ups[j] = up_ref[...]
+
+                scaled[:, :, pl.ds(j * up_rows, up_rows)] = ups[j] * adapter_scale
         if step >= 3:
             merge(step - 3)
 
@@ -258,6 +258,7 @@
         scratch_shapes=[
             pltpu.VMEM((holders * layers * kinds, rank, columns), down.dtype),
             pltpu.VMEM((train,) + up.shape, up.dtype),
+            pltpu.VMEM(weight.shape[:3] + (rank,), up.dtype),
             pltpu.SemaphoreType.DMA((holders * kinds,)),
             pltpu.SemaphoreType.DMA((holders * kinds,)),
             pltpu.SemaphoreType.DMA((2,)),

time: 41.3 us -> 37.7 us (0.913)
  Pallas kernels: 35.9 us -> 32.3 us
    pallas_call x1, Pallas kernels: 35.9 us -> 32.3 us  [relayed(): pl.pallas_call(kernel, out_shape=pltpu.VMEM(weight.shape, weight.dtype),...]
where the time goes in v2:
time: 37.7 us; the launch traced here: 37.5 us
  Pallas kernels  32.3 us (86%)
  local copies, waits for them, and re-layouts  5.19 us (14%)
    pallas_call x1, Pallas kernels, relayed(): pl.pallas_call(kernel, out_shape=pltpu.VMEM(weight.shape, weight.dtype),...  32.3 us
    unnamed x5, local copies, waits for them, and re-layouts  5.19 us

profile of v2, /device:TPU:0, one launch (start us, length us, event | category | flops | bytes accessed | tf_op | source)
XLA Modules:
  0.0 37.5 jit_solution(7186975118479942930)
XLA Ops:
  0.0 0.0 copy-start
  0.0 0.9 %copy-done = bf16[2,2,64,512]{3,2,1,0:T(8,128)(2,1)S(1)} copy-done((bf16[2,2,64,512]{3,2,1,0:T(8,128)(2,1)S(1)}, bf16[2,2,64,512]{3,2,1,0:T(8,128)(2,1)}, u32[]{:S(2)}) %copy-start) | copy-done | bytes 262168
  1.0 0.0 copy-start.1
  1.0 0.8 %copy-done.1 = bf16[2,2,64,64]{3,2,1,0:T(8,128)(2,1)S(1)} copy-done((bf16[2,2,64,64]{3,2,1,0:T(8,128)(2,1)S(1)}, bf16[2,2,64,64]{3,2,1,0:T(8,128)(2,1)}, u32[]{:S(2)}) %copy-start.1) | copy-done | bytes 32792
  1.8 32.3 %gather_merge.1 = bf16[2,2,128,8192]{3,2,1,0:T(8,128)(2,1)S(1)} custom-call(bf16[2,2,64,512]{3,2,1,0:T(8,128)(2,1)S(1)} %copy-done, bf16[2,2,64,64]{3,2,1,0:T(8,128)(2,1)S(1)} %copy-done.1, bf16[2,2,128,8192]{3,2,1,0:T(8,128)(2,1)} %weight_ref.1), custom_call_target="tpu_custom_call" | custom-call | tf_op jit(solution)/shard_map/gather_merge/pallas_call | solution.py:253
  34.1 3.4 %copy.5 = bf16[2,2,128,8192]{3,2,1,0:T(8,128)(2,1)} copy(bf16[2,2,128,8192]{3,2,1,0:T(8,128)(2,1)S(1)} %gather_merge.1) | data formatting | bytes 16777216
Async XLA Ops:
  0.0 0.9 %copy-start = (bf16[2,2,64,512]{3,2,1,0:T(8,128)(2,1)S(1)}, bf16[2,2,64,512]{3,2,1,0:T(8,128)(2,1)}, u32[]{:S(2)}) copy-start(bf16[2,2,64,512]{3,2,1,0:T(8,128)(2,1)} %down_ref.1) | copy-start | bytes 786436
  1.0 0.8 %copy-start.1 = (bf16[2,2,64,64]{3,2,1,0:T(8,128)(2,1)S(1)}, bf16[2,2,64,64]{3,2,1,0:T(8,128)(2,1)}, u32[]{:S(2)}) copy-start(bf16[2,2,64,64]{3,2,1,0:T(8,128)(2,1)} %up_ref.1) | copy-start | bytes 98308
